TPU v7x, 256 devices: a whole 4x4x8 slice. The times are simulated.
256 devices in a mesh: ep: 64 (over x, z, core), tp: 4 (over y).
Axes of the slice: x: 4, y: 4, z: 8, core: 2. Of those that a mesh axis runs over, the one named last changes fastest.
Arguments:
- hidden_in: bfloat16 [16384, 3584], P('ep', 'tp'), may hold values from -6 to 6
- moe_gain: bfloat16 [3584], replicated, may hold values from 0.099609375 to 1.8984375
- router_weight: bfloat16 [3584, 256], P('tp'), may hold values from -0.09375 to 0.09375
- expert_ids: int32 [16384, 8], P('ep'), may hold values from 0 to 255, all different within a row; in each aligned block of 256 rows (0 to 255, 256 to 511, ...) at most 16 rows name the same one
- shared_gate: bfloat16 [3584, 1024], P(None, 'tp'), may hold values from -0.09375 to 0.09375
- shared_up: bfloat16 [3584, 1024], P(None, 'tp'), may hold values from -0.09375 to 0.09375
- shared_down: bfloat16 [1024, 3584], P('tp'), may hold values from -0.1875 to 0.1875
- expert_gate: bfloat16 [64, 3584, 1024], P('ep', None, 'tp'), may hold values from -0.09375 to 0.09375
- expert_up: bfloat16 [64, 3584, 1024], P('ep', None, 'tp'), may hold values from -0.09375 to 0.09375
- expert_down: bfloat16 [64, 1024, 3584], P('ep', 'tp'), may hold values from -0.1875 to 0.1875
- attn_gain: bfloat16 [3584], P('tp'), may hold values from 0.099609375 to 1.8984375
- kv_down: bfloat16 [3584, 576], P('tp'), may hold values from -0.09375 to 0.09375
- kv_gain: bfloat16 [512], replicated, may hold values from 0.099609375 to 1.8984375
- doc_lengths: int32 [64, 4], P('ep'), may hold values from 1 to 128, 256 in all within a row
- page_table: int32 [64, 4], P('ep'), may hold values from 0 to 3, each once within a row
Outputs:
- layer_out: bfloat16 [16384, 3584], P('ep', 'tp')
- kv_pages: bfloat16 [64, 4, 64, 576], P('ep', 'tp')
Inputs may be any that keep to these rules, and one draw needn't show every extreme that they name: `expert_ids`: each row names 8 different experts. Among the rows of one ep index no expert is named more than 16 times. `doc_lengths`: each row sums to 256. `page_table`: each row holds every number below 4 once.
All inputs are finite; a program needn't handle non-finite values.
Results may differ from a plain program's by a relative error of at most 0.0065.
Values may be sent and summed in bfloat16 or wider, within the bound.
A program may use at most 128 MiB of HBM per device.

v0:
```python
import math

import jax
import jax.numpy as jnp
from jax import lax
from jax.sharding import PartitionSpec as P

CAP = 16
KVR = 512


EPS = 1e-06
ROUTE_SCALE = 2.5
THETA = 10000.0


def split_up(value, dim, length):
    dims = value.shape
    pieces = value.reshape(*dims[:dim], length, dims[dim] // length, *dims[dim + 1 :])
    return jnp.moveaxis(pieces, dim, 0)


def sum_at_owner(value, axis, dim):
    length = lax.axis_size(axis)
    pieces = lax.all_to_all(split_up(value, dim, length), axis, 0, 0, tiled=True)
    return jnp.sum(pieces, axis=0)


def sent_together(arrays, axis, dim, along):
    widths = [math.prod(a.shape[along:]) for a in arrays]
    both = jnp.concatenate(
        [a.reshape(*a.shape[:along], w) for a, w in zip(arrays, widths)], axis=along
    )
    whole = sum_at_owner(both, axis, dim)
    pieces = jnp.split(whole, [sum(widths[:k]) for k in range(1, len(widths))], axis=along)
    return tuple(
        (b.reshape(*whole.shape[:along], *a.shape[along:]) for a, b in zip(arrays, pieces))
    )


def silu(values):
    return values / (1.0 + jnp.exp(-values))


def route_weights(logits, expert_ids):
    scores = 1.0 / (1.0 + jnp.exp(-logits))
    picked = jnp.take_along_axis(scores, expert_ids, axis=1)
    return ROUTE_SCALE * picked / jnp.sum(picked, axis=1, keepdims=True)


def slot_table(expert_ids, gate_weights, expert_count, capacity):
    token_count = expert_ids.shape[0]
    columns = jnp.arange(expert_count, dtype=jnp.int32)
    matched = expert_ids[:, :, None] == columns[None, None, :]
    weight_rows = jnp.sum(jnp.where(matched, gate_weights[:, :, None], 0.0), axis=1)
    chosen = jnp.any(matched, axis=1).astype(jnp.int32)
    before = jnp.cumsum(chosen, axis=0) - chosen
    target = jnp.where(chosen > 0, columns[None, :] * capacity + before, expert_count * capacity)
    token_index = jnp.broadcast_to(jnp.arange(token_count, dtype=jnp.int32)[:, None], target.shape)
    slot_token = (
        jnp.full((expert_count * capacity + 1,), token_count, jnp.int32)
        .at[target.reshape(-1)]
        .set(token_index.reshape(-1))
    )
    slot_weight = (
        jnp.zeros((expert_count * capacity + 1,), jnp.float32)
        .at[target.reshape(-1)]
        .set(weight_rows.reshape(-1))
    )
    return (slot_token[:-1], slot_weight[:-1])


def positions_of(lengths, token_count):
    doc_ends = jnp.cumsum(lengths)
    doc_starts = doc_ends - lengths
    token_index = jnp.arange(token_count, dtype=jnp.int32)
    doc_begin = jnp.max(
        jnp.where(doc_starts[None, :] <= token_index[:, None], doc_starts[None, :], 0), axis=1
    )
    return (token_index - doc_begin).astype(jnp.float32)


def rotate(rope_part, position):
    half_width = rope_part.shape[1] // 2
    frequency = THETA ** (-jnp.arange(half_width, dtype=jnp.float32) * 2.0 / rope_part.shape[1])
    angles = position[:, None] * frequency[None, :]
    cosine = jnp.cos(angles)
    sine_part = jnp.sin(angles)
    first_half = rope_part[:, :half_width]
    second_half = rope_part[:, half_width:]
    return jnp.concatenate(
        [
            first_half * cosine - second_half * sine_part,
            second_half * cosine + first_half * sine_part,
        ],
        axis=1,
    )


def finish(latent, position, kv_gain):
    plain_part = latent[:, :KVR]
    row_scale = lax.rsqrt(jnp.mean(plain_part * plain_part, axis=1, keepdims=True) + EPS)
    normed = plain_part * row_scale * kv_gain.astype(jnp.float32)
    return jnp.concatenate([normed, rotate(latent[:, KVR:], position)], axis=1).astype(jnp.bfloat16)


def per_device(
    hidden_in,
    moe_gain,
    router_weight,
    expert_ids,
    shared_gate,
    shared_up,
    shared_down,
    expert_gate,
    expert_up,
    expert_down,
    attn_gain,
    kv_down,
    kv_gain,
    doc_lengths,
    page_table,
):
    groups = lax.axis_size("ep")
    tp_count = lax.axis_size("tp")
    member = lax.axis_index("tp")
    tok_rows, width_local = hidden_in.shape
    full_width = width_local * tp_count
    capacity = CAP
    gathered = lax.all_gather(hidden_in, "tp", axis=1, tiled=True)
    stream = gathered.astype(jnp.float32)
    inverse = lax.rsqrt(jnp.mean(stream * stream, axis=1, keepdims=True) + EPS)
    normed = (stream * inverse * moe_gain.astype(jnp.float32)).astype(jnp.bfloat16)
    normed_local = lax.dynamic_slice_in_dim(normed, member * width_local, width_local, 1)
    logits = lax.psum(
        jnp.dot(normed_local, router_weight, preferred_element_type=jnp.float32).astype(
            jnp.bfloat16
        ),
        "tp",
    ).astype(jnp.float32)
    gate_weights = route_weights(logits, expert_ids)
    slot_token, slot_weight = slot_table(expert_ids, gate_weights, groups, capacity)
    shared_hidden = (
        silu(jnp.dot(normed, shared_gate, preferred_element_type=jnp.float32))
        * jnp.dot(normed, shared_up, preferred_element_type=jnp.float32)
    ).astype(jnp.bfloat16)
    shared_part = jnp.dot(shared_hidden, shared_down, preferred_element_type=jnp.float32)
    w_gate = expert_gate[0]
    w_up = expert_up[0]
    w_down = expert_down[0]
    padded = jnp.concatenate([normed_local, jnp.zeros((1, width_local), jnp.bfloat16)], axis=0)
    send_rows = padded[slot_token].reshape(groups, capacity, width_local)
    arrived = lax.all_to_all(send_rows, "ep", split_axis=0, concat_axis=0, tiled=True)
    row_count = groups * capacity
    piece_rows = lax.all_gather(arrived, "tp", axis=2, tiled=True)
    piece_width = piece_rows.shape[2]
    flat_rows = piece_rows.reshape(row_count, piece_width)
    gate_sum = jnp.dot(flat_rows, w_gate, preferred_element_type=jnp.float32)
    up_sum = jnp.dot(flat_rows, w_up, preferred_element_type=jnp.float32)
    hidden_rows = (silu(gate_sum) * up_sum).astype(jnp.bfloat16)
    outputs = jnp.dot(hidden_rows, w_down, preferred_element_type=jnp.float32).reshape(
        groups, capacity, full_width
    )
    reduced = lax.psum_scatter(outputs, "tp", scatter_dimension=2, tiled=True)
    returned = lax.all_to_all(reduced, "ep", split_axis=0, concat_axis=0, tiled=True)
    weighted = returned.reshape(groups * capacity, width_local) * slot_weight[:, None]
    routed = jax.ops.segment_sum(weighted, slot_token, num_segments=tok_rows + 1)[:tok_rows]
    branch_sum = sum_at_owner(shared_part, "tp", 1) + routed
    layer_out = (hidden_in.astype(jnp.float32) + branch_sum).astype(jnp.bfloat16)
    out_values = layer_out.astype(jnp.float32)
    scaled = (out_values * attn_gain.astype(jnp.float32)).astype(jnp.bfloat16)
    latent_part = jnp.dot(scaled, kv_down, preferred_element_type=jnp.float32)
    squares = jnp.sum(out_values * out_values, axis=1)
    positions = positions_of(doc_lengths[0], tok_rows)
    page_count = page_table.shape[1]
    per_owner = page_count // tp_count
    page_len = tok_rows // page_count
    own_slots = lax.dynamic_slice_in_dim(page_table[0], member * per_owner, per_owner, 0)
    share_rows = tok_rows // tp_count
    latent_sum, energy = sent_together((latent_part, squares), "tp", 0, 1)
    latent = latent_sum * lax.rsqrt(energy / full_width + EPS)[:, None]
    own_cache = finish(
        latent, lax.dynamic_slice_in_dim(positions, member * share_rows, share_rows, 0), kv_gain
    )
    all_cache = lax.all_gather(own_cache, "tp", axis=0, tiled=True)
    cache_rows = all_cache.reshape(page_count, page_len, -1)[own_slots]
    page_out = cache_rows.reshape(1, per_owner, page_len, cache_rows.shape[-1])
    return (layer_out, page_out)


def solution(mesh):
    placed = (
        P("ep", "tp"),
        P(),
        P("tp", None),
        P("ep", None),
        P(None, "tp"),
        P(None, "tp"),
        P("tp", None),
        P("ep", None, "tp"),
        P("ep", None, "tp"),
        P("ep", "tp", None),
        P("tp"),
        P("tp", None),
        P(),
        P("ep", None),
        P("ep", None),
    )
    return jax.shard_map(
        per_device,
        mesh=mesh,
        in_specs=placed,
        out_specs=(P("ep", "tp"), P("ep", "tp", None, None)),
        check_vma=False,
    )
```

profile of v0, /device:TPU:1, one launch (start us, length us, event | category | flops | bytes accessed | tf_op | source)
XLA Modules:
  0.0 590.3 jit_solution(2559080063956350363)
XLA Ops:
  10.8 60.3 %scatter_custom_fusion = s32[1025]{0:T(1024)S(1)} fusion(s32[16384]{0:T(1024)S(1)} %bitcast.77, s32[16384]{0:T(1024)S(1)} %reshape.193, s32[]{:T(128)} %constant.30.clone.1), kind=kCustom, calls=%fused_computation.84 | custom fusion | bytes 4104 | tf_op jit(solution)/shard_map/scatter | solution.py:63
  71.2 2.1 fusion
  75.1 5.3 gather_fusion
  80.4 58.5 %all_to_all.20 = bf16[64,16,896]{2,1,0:T(8,128)(2,1)} all-to-all(bf16[64,16,896]{2,1,0:T(8,128)(2,1)} %bitcast.72), channel_id=1, replica_groups=mesh['ep'=64,'tp'=4] {'ep'}, dimensions={0} | all-to-all | bytes 3670016 | tf_op jit(solution)/shard_map/all_to_all | solution.py:153
  138.9 73.7 %all-gather.5.cloned.1.call-done = bf16[64,16,3584]{2,1,0:T(8,128)(2,1)} async-done(((bf16[64,16,896]{2,1,0:T(8,128)(2,1)}), bf16[64,16,3584]{2,1,0:T(8,128)(2,1)}) %all-gather.5.cloned.1.call-update) | async-done | bytes 7340048 | tf_op jit(solution)/shard_map/all_gather | solution.py:155
  212.6 5.8 fusion.7
  218.8 2.1 fusion.12
  220.9 7.3 %fusion.3 = f32[64,16,3584]{2,1,0:T(8,128)} fusion(bf16[64,16,256]{2,1,0:T(8,128)(2,1)S(1)} %bitcast.74, bf16[1,256,3584]{2,1,0:T(8,128)(2,1)S(1)} %copy-done), kind=kOutput, calls=%fused_computation.12 | convolution fusion | flops 1879048192 | bytes 17039360 | tf_op jit(solution)/shard_map/dot_general | solution.py:161
  229.7 2.1 fusion.53
  231.8 6.0 %fusion.16 = f32[256,3584]{1,0:T(8,128)} fusion(bf16[256,3584]{1,0:T(8,128)(2,1)} %param.21, bf16[256,3584]{1,0:T(8,128)(2,1)S(1)} %copy-done.3, bf16[3584,256]{1,0:T(8,128)(2,1)} %param.20, f32[256,256]{1,0:T(8,128)S(1)} %fusion.53), kind=kOutput, calls=%fused_computation.25 | convolution fusion | flops 939851776 | bytes 9437184 | tf_op jit(solution)/shard_map/dot_general | solution.py:147
  237.8 2.3 copy.95
  240.1 85.8 %all_to_all.21 = f32[4,256,896]{2,1,0:T(8,128)} all-to-all(f32[4,256,896]{2,1,0:T(8,128)S(1)} %bitcast.71), channel_id=1, replica_groups=mesh['ep'=64,'tp'=4] {'tp'}, dimensions={0} | all-to-all | bytes 7340032 | tf_op jit(solution)/shard_map/all_to_all | solution.py:25
  326.0 76.7 %reduce-scatter.2.cloned.1.call-done = f32[64,16,896]{2,1,0:T(8,128)} async-done(((f32[64,16,3584]{2,1,0:T(8,128)}), f32[64,16,896]{2,1,0:T(8,128)}) %reduce-scatter.2.cloned.1.call-update) | async-done | bytes 3670032 | tf_op jit(solution)/shard_map/reduce_scatter | solution.py:164
  402.7 10.9 %all-to-all-start.2 = ((f32[64,16,896]{2,1,0:T(8,128)}), f32[64,16,896]{2,1,0:T(8,128)}, u32[]{:S(2)}, u32[]{:S(2)}) async-start(f32[64,16,896]{2,1,0:T(8,128)} %reduce-scatter.2.cloned.1.call-done), calls=%async_computation.3 | async-start | bytes 7340032 | tf_op jit(solution)/shard_map/all_to_all | solution.py:165
  417.7 44.4 %all-reduce.3.cloned.1.call-done = bf16[256,256]{1,0:T(8,128)(2,1)} async-done(((bf16[256,256]{1,0:T(8,128)(2,1)}), bf16[256,256]{1,0:T(8,128)(2,1)}) %all-reduce.3.cloned.1.call-update) | async-done | bytes 131088 | tf_op jit(solution)/shard_map/psum | solution.py:135
  463.1 16.6 %gather_fusion.1 = f32[2048]{0:T(1024)S(1)} fusion(f32[256,256]{1,0:T(8,128)S(1)} %add_divide_fusion, s32[2048]{0:T(1024)S(1)} %reshape.183), kind=kCustom, calls=%fused_computation.1 | custom fusion | bytes 32768 | tf_op jit(solution)/shard_map/jit(take_along_axis)/gather | solution.py:47
  480.2 60.3 %scatter_custom_fusion.1 = f32[1025]{0:T(1024)S(1)} fusion(s32[16384]{0:T(1024)S(1)} %bitcast.78, f32[16384]{0:T(1024)S(1)} %reshape.201, f32[]{:T(128)} %constant.26.clone.1), kind=kCustom, calls=%fused_computation.82 | custom fusion | bytes 4104 | tf_op jit(solution)/shard_map/scatter | solution.py:68
  540.5 2.3 reduce_sum.64
  542.9 4.2 bitcast_multiply_fusion
  547.1 10.4 %scatter_custom_fusion.2 = f32[257,896]{1,0:T(8,128)S(1)} fusion(s32[1024]{0:T(1024)S(1)} %get-tuple-element.18, f32[1024,896]{1,0:T(8,128)} %bitcast_multiply_fusion, f32[]{:T(128)} %constant.26.clone.1), kind=kCustom, calls=%fused_computation.35 | custom fusion | flops 917504 | bytes 921600 | tf_op jit(solution)/shard_map/scatter-add | solution.py:167
  558.1 1.8 fusion.24
  560.8 3.5 all-to-all-start.3
  564.5 8.1 %all-to-all-done.3 = f32[4,64,577]{2,1,0:T(8,128)S(1)} async-done(((f32[4,64,577]{2,1,0:T(8,128)}), f32[4,64,577]{2,1,0:T(8,128)S(1)}, u32[]{:S(2)}, u32[]{:S(2)}) %all-to-all-start.3) | async-done | bytes 590880 | tf_op jit(solution)/shard_map/all_to_all | solution.py:25
  573.6 9.5 %all_gather.11 = bf16[256,576]{1,0:T(8,128)(2,1)S(1)} all-gather(bf16[64,576]{1,0:T(8,128)(2,1)S(1)} %copy.86), channel_id=1, replica_groups=mesh['ep'=64,'tp'=4] {'tp'}, dimensions={0}, use_global_device_ids=true | all-gather | bytes 368640 | tf_op jit(solution)/shard_map/all_gather | solution.py:185
  (95 shorter events, 14.0 us)
Async XLA Ops:
  7.2 213.7 %copy-start = (bf16[1,256,3584]{2,1,0:T(8,128)(2,1)S(1)}, bf16[1,256,3584]{2,1,0:T(8,128)(2,1)}, u32[]{:S(2)}) copy-start(bf16[1,256,3584]{2,1,0:T(8,128)(2,1)} %param.24) | copy-start | bytes 5505028
  7.2 64.0 %all-gather.3.cloned.1.call-start = ((), (), s32[]{:S(2)}) async-start(), calls=%async_computation.5 | async-start | bytes 2293760 | tf_op jit(solution)/shard_map/all_gather | solution.py:130
  7.9 204.7 %all-gather.5.cloned.1.call-start = ((), (), s32[]{:S(2)}) async-start(), calls=%async_computation.6 | async-start | bytes 9175040 | tf_op jit(solution)/shard_map/all_gather | solution.py:155
  71.2 2.1 copy-start.4
  73.8 1.2 copy-start.2
  138.9 263.8 %reduce-scatter.2.cloned.1.call-start = ((), (), s32[]{:S(2)}) async-start(), calls=%async_computation.7 | async-start | bytes 18350080 | tf_op jit(solution)/shard_map/reduce_scatter | solution.py:164
  212.6 5.8 copy-start.11
  212.6 6.2 %copy-start.12 = (bf16[1,3584,256]{2,1,0:T(8,128)(2,1)S(1)}, bf16[1,3584,256]{2,1,0:T(8,128)(2,1)}, u32[]{:S(2)}) copy-start(bf16[1,3584,256]{2,1,0:T(8,128)(2,1)} %param.23) | copy-start | bytes 5505028
  228.2 1.5 copy-start.3
  325.9 87.7 %copy-start.13 = (s32[1,4]{1,0:T(1,128)S(1)}, s32[1,4]{1,0:T(1,128)}, u32[]{:S(2)}) copy-start(s32[1,4]{1,0:T(1,128)} %param.29) | copy-start | bytes 52
  325.9 89.6 %copy-start.14 = (s32[1,4]{1,0:T(1,128)S(1)}, s32[1,4]{1,0:T(1,128)}, u32[]{:S(2)}) copy-start(s32[1,4]{1,0:T(1,128)} %param.28) | copy-start | bytes 52
  325.9 89.8 %copy-start.10 = (bf16[512]{0:T(512)(128)(2,1)S(1)}, bf16[512]{0:T(512)(128)(2,1)}, u32[]{:S(2)}) copy-start(bf16[512]{0:T(512)(128)(2,1)} %param.27) | copy-start | bytes 3076
  325.9 89.8 %copy-start.9 = (bf16[896]{0:T(1024)(128)(2,1)S(1)}, bf16[896]{0:T(1024)(128)(2,1)}, u32[]{:S(2)}) copy-start(bf16[896]{0:T(1024)(128)(2,1)} %param.25) | copy-start | bytes 5380
  325.9 89.8 %copy-start.8 = (s32[256,8]{0,1:T(8,128)S(1)}, s32[256,8]{0,1:T(8,128)}, u32[]{:S(2)}) copy-start(s32[256,8]{0,1:T(8,128)} %param.18) | copy-start | bytes 24580
  326.0 90.7 %copy-start.7 = (bf16[896,256]{1,0:T(8,128)(2,1)S(1)}, bf16[896,256]{1,0:T(8,128)(2,1)}, u32[]{:S(2)}) copy-start(bf16[896,256]{1,0:T(8,128)(2,1)} %param.17) | copy-start | bytes 1376260
  402.7 140.2 %all-to-all-start.2 = ((f32[64,16,896]{2,1,0:T(8,128)}), f32[64,16,896]{2,1,0:T(8,128)}, u32[]{:S(2)}, u32[]{:S(2)}) async-start(f32[64,16,896]{2,1,0:T(8,128)} %reduce-scatter.2.cloned.1.call-done), calls=%async_computation.3 | async-start | bytes 7340032 | tf_op jit(solution)/shard_map/all_to_all | solution.py:165
  413.6 48.5 %all-reduce.3.cloned.1.call-start = ((), (), s32[]{:S(2)}) async-start(), calls=%async_computation.8 | async-start | bytes 262144 | tf_op jit(solution)/shard_map/psum | solution.py:135
  542.9 14.7 %copy-start.5 = (bf16[256,896]{1,0:T(8,128)(2,1)S(1)}, bf16[256,896]{1,0:T(8,128)(2,1)}, u32[]{:S(2)}) copy-start(bf16[256,896]{1,0:T(8,128)(2,1)} %param.15) | copy-start | bytes 1376260
  557.8 3.0 copy-start.6
  560.8 11.8 %all-to-all-start.3 = ((f32[4,64,577]{2,1,0:T(8,128)}), f32[4,64,577]{2,1,0:T(8,128)S(1)}, u32[]{:S(2)}, u32[]{:S(2)}) async-start(f32[4,64,577]{2,1,0:T(8,128)} %pad_maximum_fusion), calls=%async_computation.4 | async-start | bytes 1310720 | tf_op jit(solution)/shard_map/all_to_all | solution.py:25
  564.5 19.2 %copy-start.1 = (bf16[1,256,3584]{2,1,0:T(8,128)(2,1)S(1)}, bf16[1,256,3584]{2,1,0:T(8,128)(2,1)}, u32[]{:S(2)}) copy-start(bf16[1,256,3584]{2,1,0:T(8,128)(2,1)} %param.24) | copy-start | bytes 5505028
Sparse Core Ops, SparseCore 0:
  9.8 34.8 all-gather.2
  139.0 73.5 all-gather.4
  228.3 174.3 reduce-scatter.1
  417.8 44.2 all-reduce.2
where the time goes:
time: 596 us; the launch traced here: 590 us
  waiting for transfers between devices  204 us (34%)
  blocking collectives  154 us (26%)
  local copies, waits for them, and re-layouts  151 us (25%)
  matrix products  26.1 us (4%)
  other arithmetic  25.1 us (4%)
  between operations  16.2 us (3%)
  starting transfers between devices  14.5 us (2%)
    all_to_all x1, blocking collectives, sum_at_owner(): lax.all_to_all(split_up(value, dim, length), axis, 0, 0, tiled=True)  85.8 us
    reduce_scatter x1, waiting for transfers between devices, per_device(): reduced = lax.psum_scatter(outputs, 'tp', scatter_dimension=2, tiled=True)  76.7 us
    all_gather x1, waiting for transfers between devices, per_device(): piece_rows = lax.all_gather(arrived, 'tp', axis=2, tiled=True)  73.7 us
    scatter x1, local copies, waits for them, and re-layouts, slot_table(): slot_weight = jnp.zeros((expert_count * capacity + 1,), jnp.float32).at[t...  60.3 us
    scatter x1, local copies, waits for them, and re-layouts, slot_table(): slot_token = jnp.full((expert_count * capacity + 1,), token_count, jnp.in...  60.3 us
    all_to_all x1, blocking collectives, per_device(): lax.all_to_all(send_rows, 'ep', split_axis=0, concat_axis=0, tiled=True)  58.5 us
    psum x1, waiting for transfers between devices, per_device(): lax.psum(jnp.dot(normed_local, router_weight, preferred_element_type=jnp....  44.4 us
    gather x5, local copies, waits for them, and re-layouts, route_weights(): picked = jnp.take_along_axis(scores, expert_ids, axis=1)  17 us
  transfers between devices with their start and end apart: 6, of which 4 were waited for; matrix products, arithmetic and copies ran while one was open for 26% of the time, Pallas kernels for 0%

commit v1 on v0

v1 whole, which is shorter than its diff:
```python
import jax
import jax.numpy as jnp
from jax import lax
from jax.experimental import pallas as pl
from jax.experimental.pallas import tpu as pltpu
from jax.sharding import PartitionSpec as P

CAP = 16
KVR = 512
NX, NZ, NCORE, TP = 4, 8, 2, 4
PLANE = NX * NCORE
FAR = (2, 5, 6, 3, 4)
NEAR = (0, 1, 7)
NFAR, NNEAR = len(FAR), len(NEAR) * PLANE
HALF = NFAR * PLANE // 2
ORDER = (
    ("a", 2), ("a", 5), ("a", 6), ("a", 3), ("sg2",), ("s0", 2), ("s0", 5), ("sg3",), ("n", 0), ("n", 7),
    ("n", 1), ("s1", 2), ("s0", 6), ("a", 4), ("s1", 5), ("shared",), ("s0", 3), ("s2", 2), ("s2", 5),
    ("x", 0), ("s1", 3), ("s3", 2), ("x", 7), ("x", 1), ("s3", 5), ("s0", 4), ("s2", 3), ("s1", 4),
    ("s4", 5), ("s4", 2), ("s3", 3), ("s2", 4), ("s1", 6), ("s3", 4), ("s4", 3), ("s2", 6), ("s4", 4),
    ("s3", 6), ("f1",), ("s4", 6), ("f2",), ("t",),
)

EPS = 1e-06
ROUTE_SCALE = 2.5
THETA = 10000.0


def silu(values):
    return values / (1.0 + jnp.exp(-values))


def dot(a, b):
    return jnp.dot(a, b, preferred_element_type=jnp.float32)


def positions_of(lengths, tokens):
    doc_ends = jnp.cumsum(lengths)
    doc_starts = doc_ends - lengths
    doc_begin = jnp.max(
        jnp.where(doc_starts[None, :] <= tokens[:, None], doc_starts[None, :], 0), axis=1
    )
    return (tokens - doc_begin).astype(jnp.float32)


def rotate(rope_part, position):
    half_width = rope_part.shape[1] // 2
    frequency = THETA ** (-jnp.arange(half_width, dtype=jnp.float32) * 2.0 / rope_part.shape[1])
    angles = position[:, None] * frequency[None, :]
    cosine = jnp.cos(angles)
    sine_part = jnp.sin(angles)
    first_half = rope_part[:, :half_width]
    second_half = rope_part[:, half_width:]
    return jnp.concatenate(
        [
            first_half * cosine - second_half * sine_part,
            second_half * cosine + first_half * sine_part,
        ],
        axis=1,
    )


def finish(latent, position, kv_gain):
    plain_part = latent[:, :KVR]
    row_scale = lax.rsqrt(jnp.mean(plain_part * plain_part, axis=1, keepdims=True) + EPS)
    normed = plain_part * row_scale * kv_gain.astype(jnp.float32)
    return jnp.concatenate([normed, rotate(latent[:, KVR:], position)], axis=1).astype(jnp.bfloat16)


def turned_dot(a, b):
    return lax.dot_general(a, b, (((0,), (0,)), ((), ())), preferred_element_type=jnp.float32)


def whole_kernel(
    h_ref, ids_ref, gain_ref, router_ref, pages_ref, kv_ref,
    sg_ref, su_ref, sd_ref, eg_ref, eu_ref, ed_ref,
    out_ref, lat_ref,
    x0, xf, xd, sf, sd, p0, pf, pd, q10, q20, q1f, q2f, red, tf, td, acc, xn, hs, gs, rk, wk, pk, lt, lr,
    wg, wu, wd,
    w_sem, a_send, a_recv, g1_send, g1_recv, g2_send, g2_recv, q1_send, q1_recv, q2_send, q2_recv,
    t_send, t_recv, d_send, d_recv, b_send, b_recv, k_send, k_recv, l_send, l_recv,
):
    e = lax.axis_index("ep")
    y = lax.axis_index("tp")
    mx, mz, mc = e // (NZ * NCORE), (e // NCORE) % NZ, e % NCORE
    me = mx * NCORE + mc
    up, down, across = (y + 1) % TP, (y + TP - 1) % TP, (y + 2) % TP
    slots, cap, width = h_ref.shape
    tokens = slots * cap
    f32, bf16 = jnp.float32, jnp.bfloat16

    barrier = pltpu.get_barrier_semaphore()

    def greet(dest):
        pl.semaphore_signal(barrier, inc=1, device_id=dest, device_id_type=pl.DeviceIdType.MESH)

    for k in range(1, TP):
        greet((e, (y + k) % TP))

    def greet_expert(n, carry):
        greet(((e + n) % (NX * NZ * NCORE), y))
        return carry

    lax.fori_loop(1, NX * NZ * NCORE, greet_expert, 0)

    def remote(src, dst, send, recv, dest):
        return pltpu.make_async_remote_copy(
            src_ref=src,
            dst_ref=dst,
            send_sem=send,
            recv_sem=recv,
            device_id=dest,
            device_id_type=pl.DeviceIdType.MESH,
        )

    def ring(src, dst, send, recv, to):
        return remote(src, dst, send, recv, (e, to))

    def gather_one(c, side):
        own = xf.at[c - 1, y]
        return ring(own, own, g1_send.at[c, side], g1_recv.at[c, side], (up, down)[side])

    def gather_two(c, side):
        piece = xf.at[c - 1, (down, up)[side], pl.ds(side * (PLANE // 2), PLANE // 2)]
        return ring(piece, piece, g2_send.at[c, side], g2_recv.at[c, side], (up, down)[side])

    def reduce_one(c, side):
        piece = pf.at[c - 1, across, pl.ds(side * (PLANE // 2), PLANE // 2)]
        return ring(piece, q1f.at[c - 1, side], q1_send.at[c, side], q1_recv.at[c, side], (up, down)[side])

    def reduce_two(c, side):
        piece = pf.at[c - 1, (up, down)[side]]
        return ring(piece, q2f.at[c - 1, side], q2_send.at[c, side], q2_recv.at[c, side], (up, down)[side])

    def shared_gather_one(side):
        return ring(h_ref, x0.at[y], g1_send.at[0, side], g1_recv.at[0, side], (up, down)[side])

    def shared_gather_two(side):
        piece = x0.at[(down, up)[side], pl.ds(side * (slots // 2), slots // 2)]
        return ring(piece, piece, g2_send.at[0, side], g2_recv.at[0, side], (up, down)[side])

    def shared_reduce_one(side):
        piece = p0.at[across, pl.ds(side * (slots // 2), slots // 2)]
        return ring(piece, q10.at[side], q1_send.at[0, side], q1_recv.at[0, side], (up, down)[side])

    def shared_reduce_two(side):
        piece = p0.at[(up, down)[side]]
        return ring(piece, q20.at[side], q2_send.at[0, side], q2_recv.at[0, side], (up, down)[side])

    def picks(k):
        return ring(pk.at[y], pk.at[y], k_send.at[k], k_recv.at[k], (y + k + 1) % TP)

    def latents(k):
        to = (y + k + 1) % TP
        return ring(lt.at[to], lr.at[k], l_send.at[k], l_recv.at[k], to)

    def device(dz, i):
        return ((i // NCORE) * NZ + (mz + dz) % NZ) * NCORE + i % NCORE

    loads = [
        pltpu.make_async_copy(src, dst.at[i], w_sem.at[n])
        for n, (src, dst, i) in enumerate(
            ((sg_ref, wg, 0), (su_ref, wu, 0), (sd_ref, wd, 0), (eg_ref, wg, 1), (eu_ref, wu, 1), (ed_ref, wd, 1))
        )
    ]
    for load in loads:
        load.start()
    x0[y] = h_ref[...]

    groups = rk.shape[0]
    ids = ids_ref[...]
    top = ids.shape[0]
    expert_row = lax.broadcasted_iota(jnp.int32, (groups, tokens), 0)
    chosen = jnp.zeros((groups, tokens), f32)
    for k in range(top):
        chosen = jnp.where(ids[k : k + 1, :] == expert_row, 1.0, chosen)
    earlier = lax.broadcasted_iota(jnp.int32, (tokens, tokens), 0)
    later = lax.broadcasted_iota(jnp.int32, (tokens, tokens), 1)
    before = dot(chosen.astype(bf16), jnp.where(earlier < later, 1.0, 0.0).astype(bf16))
    rk[...] = jnp.where(chosen > 0.0, before, -1.0)
    place = lax.broadcasted_iota(jnp.int32, (cap, tokens), 0).astype(f32)

    def one_hot(s, expert):
        gs[pl.ds(s * cap, cap), :] = jnp.where(rk[pl.ds(expert, 1), :] == place, 1.0, 0.0).astype(bf16)

    def weighted(s, expert):
        gs[pl.ds(s * cap, cap), :] = jnp.where(
            rk[pl.ds(expert, 1), :] == place, wk[pl.ds(expert, 1), :], 0.0
        ).astype(bf16)

    def all_peers(send, skip_self=False):
        def body(n, carry):
            send((me + n) % PLANE)
            return carry

        lax.fori_loop(1 if skip_self else 0, PLANE, body, 0)

    for q, dz in enumerate(FAR):
        for i in range(PLANE):
            one_hot(i, device(dz, i))
        sf[q] = (
            dot(gs[0 : PLANE * cap, :], h_ref[...].reshape(tokens, width))
            .astype(bf16)
            .reshape(PLANE, cap, width)
        )

    pl.semaphore_wait(barrier, NX * NZ * NCORE - 1 + TP - 1)
    for side in range(2):
        shared_gather_one(side).start()

    def far_rows(dz):
        q = FAR.index(dz)

        def straight(i):
            remote(sf.at[q, i], xf.at[q, y, me], a_send, a_recv.at[q], (device(dz, i), y)).start()

        all_peers(straight)

    def norm(count, piece):
        def body(i, carry):
            parts = [piece(i, j).astype(f32) for j in range(TP)]
            energy = sum(jnp.sum(v * v, axis=1, keepdims=True) for v in parts)
            inverse = lax.rsqrt(energy / (width * TP) + EPS)
            at = pl.ds(pl.multiple_of(i * cap, cap), cap)
            for j in range(TP):
                xn[at, j * width : (j + 1) * width] = (
                    parts[j] * inverse * gain_ref[:, j * width : (j + 1) * width]
                ).astype(bf16)
            return carry

        lax.fori_loop(0, count, body, 0)

    def units(rows, w):
        a = xn[0:rows, :]
        hs[0:rows, :] = (silu(dot(a, wg[w])) * dot(a, wu[w])).astype(bf16)

    def down_part(rows, w, j):
        return dot(hs[0:rows, :], wd[w, :, j * width : (j + 1) * width])

    def near_rows(dz):
        k = NEAR.index(dz)
        for i in range(PLANE):
            one_hot(i, device(dz, i))
        for j in range(TP):
            part = dot(gs[0 : PLANE * cap, :], x0[j].reshape(tokens, width)).astype(bf16)
            sd[k * PLANE : (k + 1) * PLANE, j] = part.reshape(PLANE, cap, width)

        def send(i):
            remote(
                sd.at[k * PLANE + i], xd.at[k * PLANE + me], d_send, d_recv.at[k], (device(dz, i), y)
            ).start()

        if dz == 0:
            xd[k * PLANE + me] = sd[k * PLANE + me]
        all_peers(send, dz == 0)

    def shared_part():
        norm(slots, lambda i, j: x0[j, i])
        at = pl.ds(pl.multiple_of(y * width, 128), width)
        logits = dot(xn[0:tokens, at], router_ref[...]).T
        expert = lax.broadcasted_iota(jnp.int32, logits.shape, 0)
        for k in range(top):
            pk[y, k : k + 1, :] = jnp.sum(
                jnp.where(expert == ids_ref[k : k + 1, :], logits, 0.0), axis=0, keepdims=True
            )
        for k in range(TP - 1):
            picks(k).start()
        units(tokens, 0)
        for j in range(TP):
            acc[j] = down_part(tokens, 0, j)

    def near_expert(dz):
        k = NEAR.index(dz)
        most = xd.at[pl.ds(k * PLANE, PLANE - 1 if dz == 0 else PLANE)]
        remote(most, most, d_send, d_recv.at[k], (e, up)).wait_recv()
        norm(PLANE, lambda i, j: xd[k * PLANE + i, j])
        units(PLANE * cap, 1)
        for j in range(TP):
            pd[k * PLANE : (k + 1) * PLANE, j] = (
                down_part(PLANE * cap, 1, j).astype(bf16).reshape(PLANE, cap, width)
            )

        def send_back(i):
            remote(
                pd.at[k * PLANE + i], td.at[k * PLANE + me], b_send, b_recv.at[k], (device(NZ - dz, i), y)
            ).start()

        if dz == 0:
            td[k * PLANE + me] = pd[k * PLANE + me]
        all_peers(send_back, dz == 0)

    def gather_start(c):
        remote(xf.at[c - 1, y], xf.at[c - 1, y], a_send, a_recv.at[c - 1], (e, up)).wait_recv()
        for side in range(2):
            gather_one(c, side).start()

    def gather_on(c):
        for side in range(2):
            gather_one(c, side).wait_recv()
            gather_two(c, side).start()

    def far_expert(c):
        for side in range(2):
            gather_two(c, side).wait_recv()
        norm(PLANE, lambda i, j: xf[c - 1, j, i])
        units(PLANE * cap, 1)
        for j in range(TP):
            pf[c - 1, j] = down_part(PLANE * cap, 1, j).astype(bf16).reshape(PLANE, cap, width)
        for side in range(2):
            reduce_one(c, side).start()

    def reduce_on(c):
        for side in range(2):
            reduce_one(c, side).wait_recv()
            at = pl.ds(side * (PLANE // 2), PLANE // 2)
            to = (up, down)[side]
            pf[c - 1, to, at] = (pf[c - 1, to, at].astype(f32) + q1f[c - 1, side].astype(f32)).astype(bf16)
            reduce_two(c, side).start()

    def far_back(c):
        q, dz = c - 1, FAR[c - 1]
        for side in range(2):
            reduce_two(c, side).wait_recv()
        red[q] = (pf[q, y].astype(f32) + q2f[q, 0].astype(f32) + q2f[q, 1].astype(f32)).astype(bf16)

        def straight(i):
            remote(red.at[q, i], tf.at[q * PLANE + me], t_send, t_recv, (device(NZ - dz, i), y)).start()

        all_peers(straight)

    def shared_on():
        for load in loads:
            load.wait()
        for side in range(2):
            shared_gather_one(side).wait_recv()
            shared_gather_two(side).start()

    def shared_ready():
        for side in range(2):
            shared_gather_two(side).wait_recv()

    def join_near():
        for k in range(TP - 1):
            picks(k).wait()
        scores = 1.0 / (1.0 + jnp.exp(-(pk[0] + pk[1] + pk[2] + pk[3])))
        gates = ROUTE_SCALE * scores / jnp.sum(scores, axis=0, keepdims=True)
        weights = jnp.zeros((groups, tokens), f32)
        for k in range(top):
            weights = jnp.where(ids_ref[k : k + 1, :] == expert_row, gates[k : k + 1, :], weights)
        wk[...] = weights
        for k, dz in enumerate(NEAR):
            for i in range(PLANE):
                weighted(k * PLANE + i, device(dz, i))
            most = td.at[pl.ds(k * PLANE, PLANE - 1 if dz == 0 else PLANE)]
            remote(most, most, b_send, b_recv.at[k], (e, up)).wait_recv()
        for j in range(TP):
            part = acc[j] + turned_dot(gs[0 : NNEAR * cap, :], td[:, j].reshape(NNEAR * cap, width))
            p0[j] = part.astype(bf16).reshape(slots, cap, width)
        for side in range(2):
            shared_reduce_one(side).start()

    def shared_reduce_on():
        for side in range(2):
            shared_reduce_one(side).wait_recv()
            at = pl.ds(side * (slots // 2), slots // 2)
            to = (up, down)[side]
            p0[to, at] = (p0[to, at].astype(f32) + q10[side].astype(f32)).astype(bf16)
            shared_reduce_two(side).start()

    def join_far():
        remote(tf, tf, t_send, t_recv, (e, up)).wait_recv()
        total = h_ref[...].reshape(tokens, width).astype(f32)
        for part in range(2):
            for s in range(HALF):
                slot = part * HALF + s
                weighted(s, device(FAR[slot // PLANE], slot % PLANE))
            total = total + turned_dot(
                gs[0 : HALF * cap, :], tf[part * HALF : (part + 1) * HALF].reshape(HALF * cap, width)
            )
        acc[0] = total

    steps = {
        "a": far_rows,
        "n": near_rows,
        "x": near_expert,
        "s0": lambda dz: gather_start(FAR.index(dz) + 1),
        "s1": lambda dz: gather_on(FAR.index(dz) + 1),
        "s2": lambda dz: far_expert(FAR.index(dz) + 1),
        "s3": lambda dz: reduce_on(FAR.index(dz) + 1),
        "s4": lambda dz: far_back(FAR.index(dz) + 1),
        "sg2": shared_on,
        "sg3": shared_ready,
        "shared": shared_part,
        "f1": join_near,
        "f2": shared_reduce_on,
        "t": join_far,
    }
    for name, *offset in ORDER:
        steps[name](*offset)
    for side in range(2):
        shared_reduce_two(side).wait_recv()
    total = acc[0].reshape(slots, cap, width) + p0[y].astype(f32) + q20[0].astype(f32) + q20[1].astype(f32)
    layer = total.reshape(tokens, width).astype(bf16)
    out_ref[...] = layer

    page = tokens // TP
    token = lax.broadcasted_iota(jnp.int32, (page, tokens), 1)
    inside = lax.broadcasted_iota(jnp.int32, (page, tokens), 0)
    paged = jnp.concatenate(
        [
            dot(jnp.where(token == pages_ref[0, j] * page + inside, 1.0, 0.0).astype(bf16), layer)
            for j in range(TP)
        ],
        axis=0,
    )
    energy = jnp.sum(paged * paged, axis=1, keepdims=True)
    scaled = (paged * gain_ref[:, TP * width :]).astype(bf16)
    latent = lax.dot_general(
        scaled, kv_ref[...], (((1,), (1,)), ((), ())), preferred_element_type=f32
    )
    columns = latent.shape[1]
    spare = (lt.shape[2] - columns) // 2
    coarse = energy.astype(bf16)
    fine = (energy - coarse.astype(f32)).astype(bf16)
    for j in range(TP):
        at = slice(j * page, (j + 1) * page)
        lt[j, :, 0:columns] = latent[at, :].astype(bf16)
        lt[j, :, columns : columns + spare] = jnp.broadcast_to(coarse[at, :], (page, spare))
        lt[j, :, columns + spare :] = jnp.broadcast_to(fine[at, :], (page, spare))
    for k in range(TP - 1):
        latents(k).start()
    for k in range(TP - 1):
        latents(k).wait()
    lat_ref[...] = lt[y].astype(f32) + lr[0].astype(f32) + lr[1].astype(f32) + lr[2].astype(f32)

    for side in range(2):
        shared_gather_one(side).wait_send()
        shared_gather_two(side).wait_send()
        shared_reduce_one(side).wait_send()
        shared_reduce_two(side).wait_send()

    def drain(c, carry):
        for side in range(2):
            gather_one(c, side).wait_send()
            gather_two(c, side).wait_send()
            reduce_one(c, side).wait_send()
            reduce_two(c, side).wait_send()
        return carry

    lax.fori_loop(1, NFAR + 1, drain, 0)
    remote(sf, sf, a_send, t_recv, (e, up)).wait_send()
    remote(red, red, t_send, t_recv, (e, up)).wait_send()
    most = sd.at[pl.ds(0, NNEAR - 1)]
    remote(most, most, d_send, t_recv, (e, up)).wait_send()
    remote(most, most, b_send, t_recv, (e, up)).wait_send()


def whole(hidden, ids, gain, router, pages, kv, weights):
    slots, cap, width = hidden.shape
    tokens = slots * cap
    f32, bf16 = jnp.float32, jnp.bfloat16
    hidden_units = weights[0].shape[1]
    latent = -(-(kv.shape[0] + 1) // 128) * 128
    vmem, hbm = pl.BlockSpec(memory_space=pltpu.VMEM), pl.BlockSpec(memory_space=pl.ANY)
    dma = pltpu.SemaphoreType.DMA
    pair = dma((NFAR + 1, 2))
    block = (slots, cap, width)
    strip = (PLANE, cap, width)
    return pl.pallas_call(
        whole_kernel,
        out_shape=(
            jax.ShapeDtypeStruct((tokens, width), bf16),
            jax.ShapeDtypeStruct((tokens // TP, latent), f32),
        ),
        in_specs=[vmem] * 4 + [pl.BlockSpec(memory_space=pltpu.SMEM), vmem] + [hbm] * 6,
        out_specs=(vmem, vmem),
        scratch_shapes=[
            pltpu.VMEM((TP, *block), bf16),
            pltpu.VMEM((NFAR, TP, *strip), bf16),
            pltpu.VMEM((NNEAR, TP, cap, width), bf16),
            pltpu.VMEM((NFAR, *strip), bf16),
            pltpu.VMEM((NNEAR, TP, cap, width), bf16),
            pltpu.VMEM((TP, *block), bf16),
            pltpu.VMEM((NFAR, TP, *strip), bf16),
            pltpu.VMEM((NNEAR, TP, cap, width), bf16),
            pltpu.VMEM((2, slots // 2, cap, width), bf16),
            pltpu.VMEM((2, *block), bf16),
            pltpu.VMEM((NFAR, 2, PLANE // 2, cap, width), bf16),
            pltpu.VMEM((NFAR, 2, *strip), bf16),
            pltpu.VMEM((NFAR, *strip), bf16),
            pltpu.VMEM((NFAR * PLANE, cap, width), bf16),
            pltpu.VMEM((NNEAR, TP, cap, width), bf16),
            pltpu.VMEM((TP, tokens, width), f32),
            pltpu.VMEM((tokens, width * TP), bf16),
            pltpu.VMEM((tokens, hidden_units), bf16),
            pltpu.VMEM((max(NNEAR, HALF) * cap, tokens), bf16),
            pltpu.VMEM((NX * NZ * NCORE, tokens), f32),
            pltpu.VMEM((NX * NZ * NCORE, tokens), f32),
            pltpu.VMEM((TP, *ids.shape), f32),
            pltpu.VMEM((TP, tokens // TP, latent), bf16),
            pltpu.VMEM((TP - 1, tokens // TP, latent), bf16),
            pltpu.VMEM((2, width * TP, hidden_units), bf16),
            pltpu.VMEM((2, width * TP, hidden_units), bf16),
            pltpu.VMEM((2, hidden_units, width * TP), bf16),
            dma((6,)),
            dma,
            dma((NFAR,)),
            pair, pair, pair, pair, pair, pair, pair, pair,
            dma, dma, dma, dma((len(NEAR),)), dma, dma((len(NEAR),)),
            dma((TP - 1,)), dma((TP - 1,)), dma((TP - 1,)), dma((TP - 1,)),
        ],
        compiler_params=pltpu.CompilerParams(
            collective_id=0, has_side_effects=True, vmem_limit_bytes=67000000
        ),
    )(hidden, ids, gain, router, pages, kv, *weights)


def per_device(
    hidden_in,
    moe_gain,
    router_weight,
    expert_ids,
    shared_gate,
    shared_up,
    shared_down,
    expert_gate,
    expert_up,
    expert_down,
    attn_gain,
    kv_down,
    kv_gain,
    doc_lengths,
    page_table,
):
    tp_count = lax.axis_size("tp")
    member = lax.axis_index("tp")
    tok_rows, width_local = hidden_in.shape
    full_width = width_local * tp_count
    f32 = jnp.float32
    page_count = page_table.shape[1]
    page_len = tok_rows // page_count

    layer_out, sums = whole(
        hidden_in.reshape(tok_rows // CAP, CAP, width_local),
        expert_ids.T,
        jnp.concatenate([moe_gain, attn_gain]).astype(f32).reshape(1, full_width + width_local),
        router_weight,
        page_table,
        kv_down.T,
        (shared_gate, shared_up, shared_down, expert_gate[0], expert_up[0], expert_down[0]),
    )

    slot = jnp.arange(page_count, dtype=jnp.int32)
    own_page = jnp.sum(jnp.where(slot == member, page_table[0], 0))
    tokens = own_page * page_len + jnp.arange(page_len, dtype=jnp.int32)
    columns = kv_down.shape[1]
    latent = sums[:, :columns] * lax.rsqrt(sums[:, columns : columns + 1] / full_width + EPS)
    page_out = finish(latent, positions_of(doc_lengths[0], tokens), kv_gain)
    return (layer_out, page_out.reshape(1, page_count // tp_count, page_len, -1))


def solution(mesh):
    placed = (
        P("ep", "tp"),
        P(),
        P("tp", None),
        P("ep", None),
        P(None, "tp"),
        P(None, "tp"),
        P("tp", None),
        P("ep", None, "tp"),
        P("ep", None, "tp"),
        P("ep", "tp", None),
        P("tp"),
        P("tp", None),
        P(),
        P("ep", None),
        P("ep", None),
    )
    return jax.shard_map(
        per_device,
        mesh=mesh,
        in_specs=placed,
        out_specs=(P("ep", "tp"), P("ep", "tp", None, None)),
        check_vma=False,
    )
```

time: 596 us -> 165 us (0.28)
  waiting for transfers between devices: 204 us -> 0 us
  Pallas kernels: 0 us -> 155 us
  blocking collectives: 154 us -> 0 us
  local copies, waits for them, and re-layouts: 151 us -> 3.23 us
  matrix products: 26.1 us -> 0 us
  other arithmetic: 25.1 us -> 4.62 us
  between operations: 16.2 us -> 1.37 us
  starting transfers between devices: 14.5 us -> 0 us
    pallas_call x0 -> x1, Pallas kernels: none -> 155 us  [whole(): pl.pallas_call(whole_kernel, out_shape=(jax.ShapeDtypeStruct((tokens, wid...]
    all_to_all x2 -> x0, blocking collectives: 144 us -> none  [the longest x1 85.8 us: sum_at_owner(): lax.all_to_all(split_up(value, dim, length), axis, 0, 0, tiled=True)]
    scatter x2 -> x0, local copies, waits for them, and re-layouts: 121 us -> none  [the longest x1 60.3 us: slot_table(): slot_weight = jnp.zeros((expert_count * capacity + 1,), jnp.float32).at[t...]
    reduce_scatter x1 -> x0, waiting for transfers between devices: 76.7 us -> none  [per_device(): reduced = lax.psum_scatter(outputs, 'tp', scatter_dimension=2, tiled=True)]
    all_gather x2 -> x0, waiting for transfers between devices: 73.7 us -> none  [the longest x1 73.7 us: per_device(): piece_rows = lax.all_gather(arrived, 'tp', axis=2, tiled=True)]
    psum x1 -> x0, waiting for transfers between devices: 44.4 us -> none  [per_device(): lax.psum(jnp.dot(normed_local, router_weight, preferred_element_type=jnp....]
    dot_general x7 -> x0, matrix products: 26.1 us -> none  [the longest x1 7.29 us: per_device(): jnp.dot(hidden_rows, w_down, preferred_element_type=jnp.float32)]
    gather x6 -> x0, local copies, waits for them, and re-layouts: 22.3 us -> none  [the longest x5 17 us: route_weights(): picked = jnp.take_along_axis(scores, expert_ids, axis=1)]
  transfers between devices with their start and end apart: 6 -> 0, of which waited for: 4 -> 0; matrix products, arithmetic and copies ran while one was open for 26% -> 0% of each run, Pallas kernels for 0% -> 0%
where the time goes in v1:
time: 165 us; the launch traced here: 164 us
  Pallas kernels  155 us (94%)
  other arithmetic  4.62 us (3%)
  local copies, waits for them, and re-layouts  3.23 us (2%)
    pallas_call x1, Pallas kernels, whole(): pl.pallas_call(whole_kernel, out_shape=(jax.ShapeDtypeStruct((tokens, wid...  155 us

profile of v1, /device:TPU:1, one launch (start us, length us, event | category | flops | bytes accessed | tf_op | source)
XLA Modules:
  0.0 164.4 jit_solution(12147610142222222150)
XLA Ops:
  0.6 0.7 concatenate.31
  1.3 0.7 concatenate.32
  2.0 0.6 maximum_convert_fusion.gain_ref
  2.7 0.0 copy-start
  2.7 0.0 copy-start.1
  2.7 0.0 copy-start.2
  2.7 155.2 %shard_map.158 = (bf16[256,896]{1,0:T(8,128)(2,1)}, f32[64,640]{1,0:T(8,128)}) custom-call(bf16[16,16,896]{2,1,0:T(8,128)(2,1)} %bitcast.20, s32[8,256]{1,0:T(8,128)} %bitcast.21, f32[1,4480]{1,0:T(1,128)} %maximum_convert_fusion.gain_ref, bf16[896,256]{1,0:T(8,128)(2,1)} %router_ref.1, s32[1,4]{1,0:T(1,128)} %pages_ref.1, bf16[576,896]{1,0:T(8,128)(2,1)} %bitcast.19, ...), custom_call_target="tpu_custom_call" | custom-call | tf_op jit(solution)/shard_map/pallas_call | solution.py:469
  157.9 0.9 rsqrt_reduce_fusion
  158.8 1.0 slice_multiply_fusion
  159.8 0.1 multiply_reduce_fusion
  160.0 0.0 copy-done
  160.0 0.1 fusion
  160.1 0.0 copy-done.1
  160.1 0.6 fusion.11
  161.4 0.0 copy-done.2
  161.4 0.2 reduce-window_clone.1
  161.6 0.1 select_reduce_fusion
  161.7 0.2 fusion.10
  161.9 0.7 pad_maximum_fusion
  162.6 1.8 %copy.18 = bf16[256,896]{1,0:T(8,128)(2,1)} copy(bf16[256,896]{1,0:T(8,128)(2,1)} %get-tuple-element.10) | data formatting | bytes 917504
  (6 shorter events, 0.0 us)
Async XLA Ops:
  2.7 157.3 %copy-start = (bf16[512]{0:T(512)(128)(2,1)S(1)}, bf16[512]{0:T(512)(128)(2,1)}, u32[]{:S(2)}) copy-start(bf16[512]{0:T(512)(128)(2,1)} %param.27) | copy-start | bytes 3076
  2.7 157.4 %copy-start.1 = (s32[1,4]{1,0:T(1,128)S(1)}, s32[1,4]{1,0:T(1,128)}, u32[]{:S(2)}) copy-start(s32[1,4]{1,0:T(1,128)} %pages_ref.1) | copy-start | bytes 52
  2.7 158.7 %copy-start.2 = (s32[1,4]{1,0:T(1,128)S(1)}, s32[1,4]{1,0:T(1,128)}, u32[]{:S(2)}) copy-start(s32[1,4]{1,0:T(1,128)} %param.28) | copy-start | bytes 52

commit v2 on v1

--- a/solution.py
+++ b/solution.py
@@ -9,16 +9,16 @@
 KVR = 512
 NX, NZ, NCORE, TP = 4, 8, 2, 4
 PLANE = NX * NCORE
-FAR = (2, 5, 6, 3, 4)
-NEAR = (0, 1, 7)
+FAR = (2, 7, 3, 5, 4, 6)
+NEAR = (0, 1)
 NFAR, NNEAR = len(FAR), len(NEAR) * PLANE
 HALF = NFAR * PLANE // 2
 ORDER = (
-    ("a", 2), ("a", 5), ("a", 6), ("a", 3), ("sg2",), ("s0", 2), ("s0", 5), ("sg3",), ("n", 0), ("n", 7),
-    ("n", 1), ("s1", 2), ("s0", 6), ("a", 4), ("s1", 5), ("shared",), ("s0", 3), ("s2", 2), ("s2", 5),
-    ("x", 0), ("s1", 3), ("s3", 2), ("x", 7), ("x", 1), ("s3", 5), ("s0", 4), ("s2", 3), ("s1", 4),
-    ("s4", 5), ("s4", 2), ("s3", 3), ("s2", 4), ("s1", 6), ("s3", 4), ("s4", 3), ("s2", 6), ("s4", 4),
-    ("s3", 6), ("f1",), ("s4", 6), ("f2",), ("t",),
+    ("a", 2), ("a", 7), ("a", 3), ("a", 5), ("a", 4), ("s0", 7), ("s0", 2), ("sg2",), ("a", 6), ("s1", 2),
+    ("s0", 5), ("s0", 3), ("sg3",), ("n", 1), ("s2", 2), ("n", 0), ("s1", 5), ("s0", 4), ("s3", 2),
+    ("s2", 5), ("s0", 6), ("shared",), ("s1", 4), ("s4", 2), ("s3", 5), ("s1", 3), ("x", 1), ("s1", 6),
+    ("s2", 4), ("s4", 5), ("s1", 7), ("s2", 3), ("s3", 4), ("s2", 6), ("x", 0), ("s3", 3), ("s4", 4),
+    ("s3", 6), ("s2", 7), ("f1",), ("s4", 3), ("s4", 6), ("s3", 7), ("f2",), ("s4", 7), ("t",),
 )
 
 EPS = 1e-06

time: 165 us -> 153 us (0.927)
  Pallas kernels: 155 us -> 144 us
    pallas_call x1, Pallas kernels: 155 us -> 144 us  [whole(): pl.pallas_call(whole_kernel, out_shape=(jax.ShapeDtypeStruct((tokens, wid...]
where the time goes in v2:
time: 153 us
  Pallas kernels  144 us (94%)
  other arithmetic  4.62 us (3%)
  local copies, waits for them, and re-layouts  3.23 us (2%)
    pallas_call x1, Pallas kernels, whole(): pl.pallas_call(whole_kernel, out_shape=(jax.ShapeDtypeStruct((tokens, wid...  144 us

profile of v2, /device:TPU:1, one launch (start us, length us, event | category | flops | bytes accessed | tf_op | source)
XLA Modules:
  0.0 153.0 jit_solution(14818564673708535542)
XLA Ops:
  0.6 0.7 concatenate.31
  1.3 0.7 concatenate.32
  2.0 0.6 maximum_convert_fusion.gain_ref
  2.7 0.0 copy-start
  2.7 0.0 copy-start.1
  2.7 0.0 copy-start.2
  2.7 143.8 %shard_map.158 = (bf16[256,896]{1,0:T(8,128)(2,1)}, f32[64,640]{1,0:T(8,128)}) custom-call(bf16[16,16,896]{2,1,0:T(8,128)(2,1)} %bitcast.20, s32[8,256]{1,0:T(8,128)} %bitcast.21, f32[1,4480]{1,0:T(1,128)} %maximum_convert_fusion.gain_ref, bf16[896,256]{1,0:T(8,128)(2,1)} %router_ref.1, s32[1,4]{1,0:T(1,128)} %pages_ref.1, bf16[576,896]{1,0:T(8,128)(2,1)} %bitcast.19, ...), custom_call_target="tpu_custom_call" | custom-call | tf_op jit(solution)/shard_map/pallas_call | solution.py:469
  146.5 0.9 rsqrt_reduce_fusion
  147.4 1.0 slice_multiply_fusion
  148.4 0.1 multiply_reduce_fusion
  148.5 0.0 copy-done
  148.6 0.1 fusion
  148.6 0.0 copy-done.1
  148.7 0.6 fusion.11
  150.0 0.0 copy-done.2
  150.0 0.2 reduce-window_clone.1
  150.1 0.1 select_reduce_fusion
  150.3 0.2 fusion.10
  150.5 0.7 pad_maximum_fusion
  151.2 1.8 %copy.18 = bf16[256,896]{1,0:T(8,128)(2,1)} copy(bf16[256,896]{1,0:T(8,128)(2,1)} %get-tuple-element.10) | data formatting | bytes 917504
  (6 shorter events, 0.0 us)
Async XLA Ops:
  2.7 145.9 %copy-start = (bf16[512]{0:T(512)(128)(2,1)S(1)}, bf16[512]{0:T(512)(128)(2,1)}, u32[]{:S(2)}) copy-start(bf16[512]{0:T(512)(128)(2,1)} %param.27) | copy-start | bytes 3076
  2.7 146.0 %copy-start.1 = (s32[1,4]{1,0:T(1,128)S(1)}, s32[1,4]{1,0:T(1,128)}, u32[]{:S(2)}) copy-start(s32[1,4]{1,0:T(1,128)} %pages_ref.1) | copy-start | bytes 52
  2.7 147.3 %copy-start.2 = (s32[1,4]{1,0:T(1,128)S(1)}, s32[1,4]{1,0:T(1,128)}, u32[]{:S(2)}) copy-start(s32[1,4]{1,0:T(1,128)} %param.28) | copy-start | bytes 52
